TPU v7x, 32 devices: a whole 2x2x4 slice. The times are simulated.
32 devices in a mesh: expert: 4 (over y, core), shard: 8 (over z, x).
Axes of the slice: x: 2, y: 2, z: 4, core: 2. Of those that a mesh axis runs over, the one named last changes fastest.
Arguments:
- w_gate: float32 [128, 2048, 768], P('expert', 'shard'), may hold values from -0.1875 to 0.1875
- w_up: float32 [128, 2048, 768], P('expert', 'shard'), may hold values from -0.1875 to 0.1875
- router_weight: float32 [2048, 128], P('shard', 'expert'), may hold values from -0.125 to 0.125
- router_gain: float32 [2048], P('shard'), may hold values from 0.25 to 1.75
Outputs:
- serve_gate: bfloat16 [128, 2048, 768], P('expert', None, 'shard')
- serve_up: bfloat16 [128, 2048, 768], P('expert', None, 'shard')
- scale_gate: float32 [128, 768], P('expert', 'shard')
- scale_up: float32 [128, 768], P('expert', 'shard')
- serve_router: bfloat16 [2048, 128], replicated
All inputs are finite; a program needn't handle non-finite values. Where the computation divides by a largest or mean magnitude, that divisor is 1e-20 or more.
Results may differ from a plain program's by a relative error of at most 0.001.
Values may be sent and summed in bfloat16 or wider, within the bound.
A program may use at most 192 MiB of HBM per device.

v0:
```python
import functools

import jax
import jax.numpy as jnp
from jax import lax
from jax.experimental import pallas as pl
from jax.experimental.pallas import tpu as pltpu
from jax.sharding import PartitionSpec as P

MESH = pl.DeviceIdType.MESH
SLOTS = 8
LANES = 128
NOW = 2
DIRECT = 8
EARLY = 3
CHUNK = 4


def kernel(
    n, ne,
    gate, up, router, gain,
    serve, out_scale, out_router,
    gm, ring, send, lmax, dbuf, rsbuf, half_max, xbuf, rbuf,
    load_sem, send_sem, recv_sem,
    d_send, d_recv, rs_send, rs_recv, x_send, x_recv, ag_send, ag_recv,
    r0_send, r0_recv, r1_send, r1_recv, r2_send, r2_recv,
):
    me = lax.axis_index("shard")
    my_e = lax.axis_index("expert")
    experts, rows, cols = gate.shape
    part = cols // n
    total = 2 * experts
    h = n // 2
    mine = lax.rem(me, h)
    base = me - mine
    far = (n - h) - base
    share = (total - DIRECT) // h
    peers = range(n - 1)

    def there(l):
        if l < h:
            return far + lax.rem(mine + l, h)
        return base + lax.rem(mine + (l - h + 1), h)

    def back(l):
        if l < h:
            return far + lax.rem(mine + (h - l), h)
        return base + lax.rem(mine + (2 * h - 1 - l), h)

    def near(s):
        return base + lax.rem(mine + s, h)

    def near_back(s):
        return base + lax.rem(mine + (h - s), h)

    def remote(src, dst, ssem, rsem, device):
        return pltpu.make_async_remote_copy(
            src_ref=src, dst_ref=dst, send_sem=ssem, recv_sem=rsem,
            device_id=device, device_id_type=MESH,
        )

    def load(array, index, slot):
        return pltpu.make_async_copy(array.at[index], ring.at[slot], load_sem.at[slot])

    def item_of(k):
        early = jnp.where(k < DIRECT, k, k - DIRECT)
        late = jnp.where(k < total + EARLY, k - EARLY, k - total)
        return jnp.where(k < DIRECT + EARLY, early, late)

    def fetch(k):
        slot = lax.rem(k, SLOTS)
        item = item_of(k)

        @pl.when((k < 2 * total) & (item < experts))
        def _():
            load(gate, item, slot).start()

        @pl.when((k < 2 * total) & (item >= experts))
        def _():
            load(up, item - experts, slot).start()

    for k in range(SLOTS):
        load((gate, up)[k // experts], k % experts, k).start()

    barrier = pltpu.get_barrier_semaphore()
    for l in peers:
        pl.semaphore_signal(barrier, inc=1, device_id={"shard": there(l)}, device_id_type=MESH)
    for r in range(1, ne):
        pl.semaphore_signal(
            barrier, inc=1, device_id={"expert": lax.rem(my_e + r, ne)}, device_id_type=MESH
        )

    def direct(b, l, slot):
        first, count = ((0, NOW), (NOW, DIRECT - NOW))[b]
        return remote(
            lmax.at[pl.ds(first, count)], dbuf.at[slot, pl.ds(first, count)],
            d_send.at[b, l], d_recv.at[b, l], {"shard": there(l)},
        )

    def spread(s, slot):
        return remote(
            lmax.at[pl.ds(DIRECT + lax.rem(mine + s, h) * share, share)], rsbuf.at[s],
            rs_send.at[s], rs_recv.at[s], {"shard": near(s)},
        )

    def swap():
        return remote(half_max, xbuf, x_send, x_recv, {"shard": far + mine})

    def collect(s, slot):
        block = pl.ds(DIRECT + slot * share, share)
        return remote(gm.at[block], gm.at[block], ag_send.at[s], ag_recv.at[s], {"shard": near(s)})

    def router_swap(slot):
        return remote(
            rbuf.at[my_e, me], rbuf.at[my_e, slot], r0_send, r0_recv, {"shard": far + mine}
        )

    def router_row(s, j, slot):
        return remote(
            rbuf.at[my_e, slot], rbuf.at[my_e, slot],
            r1_send.at[s, j], r1_recv.at[s, j], {"shard": near(s)},
        )

    def router_col(r, slot):
        return remote(
            rbuf.at[slot], rbuf.at[slot], r2_send.at[r], r2_recv.at[r],
            {"expert": lax.rem(my_e + r, ne)},
        )

    def column(slot):
        return pl.ds(pl.multiple_of(slot * rows, LANES), rows)

    def peer_rows(slot):
        return pl.ds(pl.multiple_of(slot * part, 16), part)

    def piece(l, slot, first, count):
        return remote(
            send.at[pl.ds(first, count), peer_rows(there(l))],
            serve.at[pl.ds(first, count), :, column(slot)],
            send_sem.at[l], recv_sem.at[l], {"shard": there(l)},
        )

    def maxima(k, item):
        slot = lax.rem(k, SLOTS)
        load(gate, 0, slot).wait()
        lmax[item] = jnp.max(jnp.abs(ring[slot]), axis=0, keepdims=True)
        fetch(k + SLOTS)

    def quotient(k, item):
        slot = lax.rem(k, SLOTS)
        load(gate, 0, slot).wait()
        inverse = 1.0 / gm[item]
        for j in range(0, cols, LANES):
            block = ring[slot, :, j:j + LANES] * inverse[:, j:j + LANES]
            send[item, j:j + LANES, :] = block.T.astype(jnp.bfloat16)
        fetch(k + SLOTS)
        serve[item, :, column(me)] = send[item, peer_rows(me), :]

    def ship(first, count):
        for l in peers:
            piece(l, me, first, count).start()

    def settle(b):
        first, count = ((0, NOW), (NOW, DIRECT - NOW))[b]
        span = pl.ds(first, count)
        largest = lmax[span]
        for l in peers:
            direct(b, l, back(l)).wait_recv()
            largest = jnp.maximum(largest, dbuf[back(l), span])
        gm[span] = largest

    def maxima_span(first, last, shift):
        @pl.loop(first, last)
        def _(item):
            maxima(item + shift, item)

    def quotient_span(first, last, shift):
        @pl.loop(first, last)
        def _(item):
            quotient(item + shift, item)
            ship(item, 1)

    maxima_span(0, NOW, 0)
    rbuf[my_e, me] = (router[...] * gain[...]).astype(jnp.bfloat16)
    pl.semaphore_wait(barrier, n + ne - 2)
    for l in peers:
        direct(0, l, me).start()
    router_swap(me).start()
    maxima_span(NOW, DIRECT, 0)
    for l in peers:
        direct(1, l, me).start()
    settle(0)
    quotient_span(0, NOW, DIRECT)
    settle(1)
    quotient_span(NOW, EARLY, DIRECT)
    maxima_span(DIRECT, total, EARLY)

    for s in range(1, h):
        spread(s, mine).start()
    quotient_span(EARLY, EARLY + 1, total)
    largest = lmax[pl.ds(DIRECT + mine * share, share)]
    for s in range(1, h):
        spread(s, mine).wait_recv()
        largest = jnp.maximum(largest, rsbuf[s])
    half_max[...] = largest
    router_swap(far + mine).wait_recv()
    swap().start()
    for s in range(1, h):
        router_row(s, 0, me).start()
        router_row(s, 1, far + mine).start()
    quotient_span(EARLY + 1, EARLY + 2, total)
    swap().wait_recv()
    gm[pl.ds(DIRECT + mine * share, share)] = jnp.maximum(half_max[...], xbuf[...])
    quotient_span(EARLY + 2, EARLY + 3, total)
    for s in range(1, h):
        collect(s, mine).start()
    quotient_span(EARLY + 3, DIRECT, total)
    for s in range(1, h):
        collect(s, lax.rem(mine + (h - s), h)).wait_recv()

    @pl.loop(0, (total - DIRECT) // CHUNK)
    def _(c):
        first = DIRECT + c * CHUNK

        @pl.loop(0, CHUNK)
        def _(i):
            quotient(total + first + i, first + i)

        @pl.when(c > 0)
        def _():
            ship(first - CHUNK, CHUNK)

    ship(total - CHUNK, CHUNK)

    for s in range(1, h):
        router_row(s, 0, near_back(s)).wait_recv()
        router_row(s, 1, far + lax.rem(mine + (h - s), h)).wait_recv()
    for r in range(1, ne):
        router_col(r, my_e).start()
    whole = gm[...].reshape(total, cols)
    for s in range(n):
        @pl.when(me == s)
        def _():
            out_scale[...] = whole[:, s * part:(s + 1) * part]
    for r in range(1, ne):
        router_col(r, lax.rem(my_e + (ne - r), ne)).wait_recv()
    for s in range(n):
        block = rbuf[:, s].astype(jnp.float32).reshape(ne * rbuf.shape[2], rows)
        out_router[s * rows:(s + 1) * rows, :] = block.T.astype(jnp.bfloat16)

    for l in peers:
        for b in range(2):
            direct(b, l, me).wait_send()
    for s in range(1, h):
        spread(s, mine).wait_send()
        collect(s, mine).wait_send()
        router_row(s, 0, me).wait_send()
        router_row(s, 1, far + mine).wait_send()
    swap().wait_send()
    router_swap(me).wait_send()
    for r in range(1, ne):
        router_col(r, my_e).wait_send()
    for l in peers:
        piece(l, me, 0, total).wait_send()
    for l in peers:
        piece(l, back(l), 0, total).wait_recv()


def place(serve, scale, router, out_gate, out_up, out_sg, out_su, out_router, sems):
    experts = out_gate.shape[0]
    moves = (
        (serve.at[pl.ds(0, experts)], out_gate),
        (serve.at[pl.ds(experts, experts)], out_up),
        (router, out_router),
        (scale.at[pl.ds(0, experts)], out_sg),
        (scale.at[pl.ds(experts, experts)], out_su),
    )
    copies = [pltpu.make_async_copy(a, b, sems.at[i]) for i, (a, b) in enumerate(moves)]
    for copy in copies:
        copy.start()
    for copy in copies:
        copy.wait()


def plain_body(w_gate, w_up, router_weight, router_gain):
    scale_gate, scale_up = lax.pmax(
        (jnp.max(jnp.abs(w_gate), axis=1), jnp.max(jnp.abs(w_up), axis=1)), "shard"
    )
    narrow_gate, narrow_up = (
        (w_gate / jnp.expand_dims(scale_gate, 1)).astype(jnp.bfloat16),
        (w_up / jnp.expand_dims(scale_up, 1)).astype(jnp.bfloat16),
    )
    serve_gate, serve_up = (
        lax.all_to_all(narrow_gate, "shard", split_axis=2, concat_axis=1, tiled=True),
        lax.all_to_all(narrow_up, "shard", split_axis=2, concat_axis=1, tiled=True),
    )
    scale_gate = lax.dynamic_slice_in_dim(
        scale_gate, lax.axis_index("shard") * serve_gate.shape[2], serve_gate.shape[2], axis=1
    )
    scale_up = lax.dynamic_slice_in_dim(
        scale_up, lax.axis_index("shard") * serve_up.shape[2], serve_up.shape[2], axis=1
    )
    part_router = (router_weight * router_gain[:, None]).astype(jnp.bfloat16)
    row_router = lax.all_gather(part_router, "shard", axis=0, tiled=True)
    serve_router = lax.all_gather(row_router, "expert", axis=1, tiled=True)
    return (serve_gate, serve_up, scale_gate, scale_up, serve_router)


def body(n, ne, w_gate, w_up, router_weight, router_gain):
    experts, rows, cols = w_gate.shape
    total, h = 2 * experts, n // 2
    fits = (
        n % 2 == 0 and rows % LANES == 0 and cols % LANES == 0 and (cols // n) % 16 == 0
        and total > DIRECT and (total - DIRECT) % h == 0 and (total - DIRECT) % CHUNK == 0
        and total >= SLOTS
    )
    if not fits:
        return plain_body(w_gate, w_up, router_weight, router_gain)
    part, share, local_e = cols // n, (total - DIRECT) // h, router_weight.shape[1]
    dma = pltpu.SemaphoreType.DMA
    anywhere = pl.BlockSpec(memory_space=pl.ANY)
    local = pl.BlockSpec(memory_space=pltpu.VMEM)
    serve, scale, router = pl.pallas_call(
        functools.partial(kernel, n, ne),
        out_shape=(
            pltpu.VMEM((total, part, n * rows), jnp.bfloat16),
            pltpu.VMEM((total, part), jnp.float32),
            pltpu.VMEM((n * rows, ne * local_e), jnp.bfloat16),
        ),
        in_specs=[anywhere, anywhere, local, local],
        out_specs=(local, local, local),
        scratch_shapes=[
            pltpu.VMEM((total, 1, cols), jnp.float32),
            pltpu.VMEM((SLOTS, rows, cols), jnp.float32),
            pltpu.VMEM((total, cols, rows), jnp.bfloat16),
            pltpu.VMEM((total, 1, cols), jnp.float32),
            pltpu.VMEM((n, DIRECT, 1, cols), jnp.float32),
            pltpu.VMEM((h, share, 1, cols), jnp.float32),
            pltpu.VMEM((share, 1, cols), jnp.float32),
            pltpu.VMEM((share, 1, cols), jnp.float32),
            pltpu.VMEM((ne, n, local_e, rows), jnp.bfloat16),
            dma((SLOTS,)),
            dma((n,)),
            dma((n,)),
            dma((2, n)),
            dma((2, n)),
            dma((h,)),
            dma((h,)),
            dma,
            dma,
            dma((h,)),
            dma((h,)),
            dma,
            dma,
            dma((h, 2)),
            dma((h, 2)),
            dma((ne,)),
            dma((ne,)),
        ],
        compiler_params=pltpu.CompilerParams(
            collective_id=0, has_side_effects=True, vmem_limit_bytes=34 * 2**20
        ),
        cost_estimate=pl.CostEstimate(
            flops=4 * experts * rows * cols, bytes_accessed=20 * experts * rows * cols, transcendentals=0
        ),
    )(w_gate, w_up, router_weight.T, router_gain[None, :])
    gate, up, scale_gate, scale_up, router = pl.pallas_call(
        place,
        out_shape=(
            pltpu.HBM((experts, part, n * rows), jnp.bfloat16),
            pltpu.HBM((experts, part, n * rows), jnp.bfloat16),
            pltpu.HBM((experts, part), jnp.float32),
            pltpu.HBM((experts, part), jnp.float32),
            pltpu.HBM((n * rows, ne * local_e), jnp.bfloat16),
        ),
        in_specs=[local] * 3,
        out_specs=(anywhere,) * 5,
        scratch_shapes=[dma((5,))],
        compiler_params=pltpu.CompilerParams(vmem_limit_bytes=2**20),
        cost_estimate=pl.CostEstimate(
            flops=0, bytes_accessed=4 * experts * rows * cols, transcendentals=0
        ),
    )(serve, scale, router)
    return (jnp.swapaxes(gate, 1, 2), jnp.swapaxes(up, 1, 2), scale_gate, scale_up, router)


def solution(mesh):
    return jax.shard_map(
        functools.partial(body, mesh.shape["shard"], mesh.shape["expert"]),
        mesh=mesh,
        in_specs=(
            P("expert", "shard", None),
            P("expert", "shard", None),
            P("shard", "expert"),
            P("shard"),
        ),
        out_specs=(
            P("expert", None, "shard"),
            P("expert", None, "shard"),
            P("expert", "shard"),
            P("expert", "shard"),
            P(),
        ),
        check_vma=False,
    )
```

profile of v0, /device:TPU:0, one launch (start us, length us, event | category | flops | bytes accessed | tf_op | source)
XLA Modules:
  0.0 567.2 jit_solution(8780001431695849812)
XLA Ops:
  0.6 557.6 %shard_map.83 = (bf16[64,96,2048]{2,1,0:T(8,128)(2,1)S(1)}, f32[64,96]{1,0:T(8,128)S(1)}, bf16[2048,128]{1,0:T(8,128)(2,1)S(1)}) custom-call(f32[32,256,768]{2,1,0:T(8,128)} %gate.1, f32[32,256,768]{2,1,0:T(8,128)} %up.1, f32[32,256]{1,0:T(8,128)} %bitcast.4, f32[1,256]{1,0:T(1,128)} %bitcast.5), custom_call_target="tpu_custom_call" | custom-call | flops 25165824 | bytes 125829120 | tf_op jit(solution)/shard_map/pallas_call | solution.py:323
  558.2 9.0 %shard_map.84 = (bf16[32,96,2048]{2,1,0:T(8,128)(2,1)}, bf16[32,96,2048]{2,1,0:T(8,128)(2,1)}, f32[32,96]{1,0:T(8,128)}, f32[32,96]{1,0:T(8,128)}, bf16[2048,128]{1,0:T(8,128)(2,1)}) custom-call(bf16[64,96,2048]{2,1,0:T(8,128)(2,1)S(1)} %get-tuple-element.13.serve, f32[64,96]{1,0:T(8,128)S(1)} %get-tuple-element.14.scale, ...), custom_call_target="tpu_custom_call" | custom-call | bytes 25165824 | tf_op jit(solution)/shard_map/pallas_call | solution.py:367
where the time goes:
time: 569 us; the launch traced here: 567 us
  Pallas kernels  567 us (100%)
    pallas_call x1, Pallas kernels, body(): pl.pallas_call(functools.partial(kernel, n, ne), out_shape=(pltpu.VMEM((t...  558 us

commit v1 on v0

--- a/solution.py
+++ b/solution.py
@@ -13,7 +13,8 @@
 NOW = 2
 DIRECT = 8
 EARLY = 3
-CHUNK = 4
+CHUNK = 2
+PLACES = 8
 
 
 def kernel(
@@ -157,7 +158,7 @@
         serve[item, :, column(me)] = send[item, peer_rows(me), :]
 
     def ship(first, count):
-        for l in peers:
+        for l in sorted(peers, key=lambda l: (l % h, l // h)):
             piece(l, me, first, count).start()
 
     def settle(b):
@@ -268,13 +269,17 @@
 
 def place(serve, scale, router, out_gate, out_up, out_sg, out_su, out_router, sems):
     experts = out_gate.shape[0]
-    moves = (
-        (serve.at[pl.ds(0, experts)], out_gate),
-        (serve.at[pl.ds(experts, experts)], out_up),
+    step = experts // PLACES
+    moves = [
+        (serve.at[pl.ds(a * experts + i * step, step)], out.at[pl.ds(i * step, step)])
+        for a, out in enumerate((out_gate, out_up))
+        for i in range(PLACES)
+    ]
+    moves += [
         (router, out_router),
         (scale.at[pl.ds(0, experts)], out_sg),
         (scale.at[pl.ds(experts, experts)], out_su),
-    )
+    ]
     copies = [pltpu.make_async_copy(a, b, sems.at[i]) for i, (a, b) in enumerate(moves)]
     for copy in copies:
         copy.start()
@@ -375,7 +380,7 @@
         ),
         in_specs=[local] * 3,
         out_specs=(anywhere,) * 5,
-        scratch_shapes=[dma((5,))],
+        scratch_shapes=[dma((2 * PLACES + 3,))],
         compiler_params=pltpu.CompilerParams(vmem_limit_bytes=2**20),
         cost_estimate=pl.CostEstimate(
             flops=0, bytes_accessed=4 * experts * rows * cols, transcendentals=0

time: 569 us -> 565 us (level)
  no operation moved by 1% of the time
where the time goes in v1:
time: 565 us
  Pallas kernels  564 us (100%)
    pallas_call x1, Pallas kernels, body(): pl.pallas_call(functools.partial(kernel, n, ne), out_shape=(pltpu.VMEM((t...  556 us

profile of v1, /device:TPU:0, one launch (start us, length us, event | category | flops | bytes accessed | tf_op | source)
XLA Modules:
  0.0 564.8 jit_solution(9694973110614616043)
XLA Ops:
  0.6 555.5 %shard_map.83 = (bf16[64,96,2048]{2,1,0:T(8,128)(2,1)S(1)}, f32[64,96]{1,0:T(8,128)S(1)}, bf16[2048,128]{1,0:T(8,128)(2,1)S(1)}) custom-call(f32[32,256,768]{2,1,0:T(8,128)} %gate.1, f32[32,256,768]{2,1,0:T(8,128)} %up.1, f32[32,256]{1,0:T(8,128)} %bitcast.4, f32[1,256]{1,0:T(1,128)} %bitcast.5), custom_call_target="tpu_custom_call" | custom-call | flops 25165824 | bytes 125829120 | tf_op jit(solution)/shard_map/pallas_call | solution.py:328
  556.1 8.7 %shard_map.84 = (bf16[32,96,2048]{2,1,0:T(8,128)(2,1)}, bf16[32,96,2048]{2,1,0:T(8,128)(2,1)}, f32[32,96]{1,0:T(8,128)}, f32[32,96]{1,0:T(8,128)}, bf16[2048,128]{1,0:T(8,128)(2,1)}) custom-call(bf16[64,96,2048]{2,1,0:T(8,128)(2,1)S(1)} %get-tuple-element.13.serve, f32[64,96]{1,0:T(8,128)S(1)} %get-tuple-element.14.scale, ...), custom_call_target="tpu_custom_call" | custom-call | bytes 25165824 | tf_op jit(solution)/shard_map/pallas_call | solution.py:372

commit v2 on v1

--- a/solution.py
+++ b/solution.py
@@ -13,6 +13,8 @@
 NOW = 2
 DIRECT = 8
 EARLY = 3
+SECOND = 16
+SHORT = 8
 CHUNK = 2
 PLACES = 8
 
@@ -20,10 +22,10 @@
 def kernel(
     n, ne,
     gate, up, router, gain,
-    serve, out_scale, out_router,
-    gm, ring, send, lmax, dbuf, rsbuf, half_max, xbuf, rbuf,
+    serve, late, out_scale, out_router,
+    gm, ring, raw, send, lmax, dbuf, ebuf, e_half, e_far, rsbuf, half_max, xbuf, rbuf,
     load_sem, send_sem, recv_sem,
-    d_send, d_recv, rs_send, rs_recv, x_send, x_recv, ag_send, ag_recv,
+    d_send, d_recv, e_send, e_recv, y_send, y_recv, rs_send, rs_recv, x_send, x_recv, ag_send, ag_recv,
     r0_send, r0_recv, r1_send, r1_recv, r2_send, r2_recv,
 ):
     me = lax.axis_index("shard")
@@ -31,6 +33,7 @@
     experts, rows, cols = gate.shape
     part = cols // n
     total = 2 * experts
+    lo, hi = total - SECOND, total - SHORT
     h = n // 2
     mine = lax.rem(me, h)
     base = me - mine
@@ -63,20 +66,23 @@
     def load(array, index, slot):
         return pltpu.make_async_copy(array.at[index], ring.at[slot], load_sem.at[slot])
 
+    again = EARLY - NOW
+    loads = 2 * total - NOW
+
     def item_of(k):
-        early = jnp.where(k < DIRECT, k, k - DIRECT)
-        late = jnp.where(k < total + EARLY, k - EARLY, k - total)
-        return jnp.where(k < DIRECT + EARLY, early, late)
+        early = jnp.where(k < DIRECT, k, k - DIRECT + NOW)
+        late = jnp.where(k < total + again, k - again, k - total + NOW)
+        return jnp.where(k < DIRECT + again, early, late)
 
     def fetch(k):
         slot = lax.rem(k, SLOTS)
         item = item_of(k)
 
-        @pl.when((k < 2 * total) & (item < experts))
+        @pl.when((k < loads) & (item < experts))
         def _():
             load(gate, item, slot).start()
 
-        @pl.when((k < 2 * total) & (item >= experts))
+        @pl.when((k < loads) & (item >= experts))
         def _():
             load(up, item - experts, slot).start()
 
@@ -91,12 +97,18 @@
             barrier, inc=1, device_id={"expert": lax.rem(my_e + r, ne)}, device_id_type=MESH
         )
 
-    def direct(b, l, slot):
-        first, count = ((0, NOW), (NOW, DIRECT - NOW))[b]
+    def direct(l, slot):
         return remote(
-            lmax.at[pl.ds(first, count)], dbuf.at[slot, pl.ds(first, count)],
-            d_send.at[b, l], d_recv.at[b, l], {"shard": there(l)},
-        )
+            lmax.at[pl.ds(0, NOW)], dbuf.at[slot], d_send.at[l], d_recv.at[l], {"shard": there(l)}
+        )
+
+    soon = pl.ds(NOW, DIRECT - NOW)
+
+    def soon_near(s):
+        return remote(lmax.at[soon], ebuf.at[s], e_send.at[s], e_recv.at[s], {"shard": near(s)})
+
+    def soon_far():
+        return remote(e_half, e_far, y_send, y_recv, {"shard": far + mine})
 
     def spread(s, slot):
         return remote(
@@ -134,41 +146,79 @@
     def peer_rows(slot):
         return pl.ds(pl.multiple_of(slot * part, 16), part)
 
-    def piece(l, slot, first, count):
+    def piece(l, slot, first, count, tail=False):
+        source = late.at[pl.ds(first - lo, count)] if tail else send.at[pl.ds(first, count)]
         return remote(
-            send.at[pl.ds(first, count), peer_rows(there(l))],
+            source.at[:, peer_rows(there(l))],
             serve.at[pl.ds(first, count), :, column(slot)],
             send_sem.at[l], recv_sem.at[l], {"shard": there(l)},
         )
 
+    def largest_of(slot, item):
+        load(gate, 0, slot).wait()
+        lmax[item] = jnp.max(jnp.abs(ring[slot]), axis=0, keepdims=True)
+
     def maxima(k, item):
         slot = lax.rem(k, SLOTS)
-        load(gate, 0, slot).wait()
-        lmax[item] = jnp.max(jnp.abs(ring[slot]), axis=0, keepdims=True)
+        largest_of(slot, item)
         fetch(k + SLOTS)
 
-    def quotient(k, item):
+    def turn(k):
+        for j in range(0, cols, LANES):
+            raw[k, j:j + LANES, :] = ring[k, :, j:j + LANES].T
+        fetch(k + SLOTS)
+
+    def quotient(k, item, tail=False):
         slot = lax.rem(k, SLOTS)
         load(gate, 0, slot).wait()
         inverse = 1.0 / gm[item]
         for j in range(0, cols, LANES):
             block = ring[slot, :, j:j + LANES] * inverse[:, j:j + LANES]
-            send[item, j:j + LANES, :] = block.T.astype(jnp.bfloat16)
+            if tail:
+                late[item - lo, j:j + LANES, :] = block.T.astype(jnp.bfloat16)
+            else:
+                send[item, j:j + LANES, :] = block.T.astype(jnp.bfloat16)
         fetch(k + SLOTS)
+        if not tail:
+            keep(item)
+
+    def keep(item):
         serve[item, :, column(me)] = send[item, peer_rows(me), :]
 
-    def ship(first, count):
+    def first_quotient(item):
+        inverse = jnp.broadcast_to(1.0 / gm[item], (8, cols))
+        for j in range(0, cols, LANES):
+            factor = inverse[:, j:j + LANES].T[:, 0:1]
+            send[item, j:j + LANES, :] = (raw[item, j:j + LANES, :] * factor).astype(jnp.bfloat16)
+        keep(item)
+        ship(item, 1)
+
+    def whole_piece(l, slot, count):
+        spot = serve.at[pl.ds(0, count), :, column(slot)]
+        return remote(spot, spot, send_sem.at[l], recv_sem.at[l], {"shard": there(l)})
+
+    def ship(first, count, tail=False):
         for l in sorted(peers, key=lambda l: (l % h, l // h)):
-            piece(l, me, first, count).start()
-
-    def settle(b):
-        first, count = ((0, NOW), (NOW, DIRECT - NOW))[b]
-        span = pl.ds(first, count)
-        largest = lmax[span]
+            piece(l, me, first, count, tail).start()
+
+    def settle_now():
+        largest = lmax[pl.ds(0, NOW)]
         for l in peers:
-            direct(b, l, back(l)).wait_recv()
-            largest = jnp.maximum(largest, dbuf[back(l), span])
-        gm[span] = largest
+            direct(l, back(l)).wait_recv()
+            largest = jnp.maximum(largest, dbuf[back(l)])
+        gm[pl.ds(0, NOW)] = largest
+
+    def settle_half():
+        largest = lmax[soon]
+        for s in range(1, h):
+            soon_near(s).wait_recv()
+            largest = jnp.maximum(largest, ebuf[s])
+        e_half[...] = largest
+        soon_far().start()
+
+    def settle_soon():
+        soon_far().wait_recv()
+        gm[soon] = jnp.maximum(e_half[...], e_far[...])
 
     def maxima_span(first, last, shift):
         @pl.loop(first, last)
@@ -181,24 +231,30 @@
             quotient(item + shift, item)
             ship(item, 1)
 
-    maxima_span(0, NOW, 0)
+    for k in range(NOW):
+        largest_of(k, k)
     rbuf[my_e, me] = (router[...] * gain[...]).astype(jnp.bfloat16)
     pl.semaphore_wait(barrier, n + ne - 2)
     for l in peers:
-        direct(0, l, me).start()
+        direct(l, me).start()
     router_swap(me).start()
+    for k in range(NOW):
+        turn(k)
     maxima_span(NOW, DIRECT, 0)
-    for l in peers:
-        direct(1, l, me).start()
-    settle(0)
-    quotient_span(0, NOW, DIRECT)
-    settle(1)
-    quotient_span(NOW, EARLY, DIRECT)
-    maxima_span(DIRECT, total, EARLY)
+    for s in range(1, h):
+        soon_near(s).start()
+    settle_now()
+    first_quotient(0)
+    settle_half()
+    for k in range(1, NOW):
+        first_quotient(k)
+    settle_soon()
+    quotient_span(NOW, EARLY, DIRECT - NOW)
+    maxima_span(DIRECT, total, again)
 
     for s in range(1, h):
         spread(s, mine).start()
-    quotient_span(EARLY, EARLY + 1, total)
+    quotient_span(EARLY, EARLY + 1, loads - total)
     largest = lmax[pl.ds(DIRECT + mine * share, share)]
     for s in range(1, h):
         spread(s, mine).wait_recv()
@@ -209,29 +265,49 @@
     for s in range(1, h):
         router_row(s, 0, me).start()
         router_row(s, 1, far + mine).start()
-    quotient_span(EARLY + 1, EARLY + 2, total)
+    quotient_span(EARLY + 1, EARLY + 2, loads - total)
     swap().wait_recv()
     gm[pl.ds(DIRECT + mine * share, share)] = jnp.maximum(half_max[...], xbuf[...])
-    quotient_span(EARLY + 2, EARLY + 3, total)
+    quotient_span(EARLY + 2, EARLY + 3, loads - total)
     for s in range(1, h):
         collect(s, mine).start()
-    quotient_span(EARLY + 3, DIRECT, total)
+    quotient_span(EARLY + 3, DIRECT, loads - total)
     for s in range(1, h):
         collect(s, lax.rem(mine + (h - s), h)).wait_recv()
 
-    @pl.loop(0, (total - DIRECT) // CHUNK)
+    @pl.loop(0, (lo - DIRECT) // CHUNK)
     def _(c):
         first = DIRECT + c * CHUNK
 
         @pl.loop(0, CHUNK)
         def _(i):
-            quotient(total + first + i, first + i)
+            quotient(loads - total + first + i, first + i)
 
         @pl.when(c > 0)
         def _():
             ship(first - CHUNK, CHUNK)
 
-    ship(total - CHUNK, CHUNK)
+    longer = lax.rem(my_e, 2) == 1
+
+    @pl.loop(0, SECOND // CHUNK)
+    def _(c):
+        first = lo + c * CHUNK
+
+        @pl.loop(0, CHUNK)
+        def _(i):
+            quotient(loads - total + first + i, first + i, True)
+
+        @pl.when(c == 0)
+        def _():
+            ship(lo - CHUNK, CHUNK)
+
+        @pl.when((c > 0) & (first <= hi) & longer)
+        def _():
+            ship(first - CHUNK, CHUNK, True)
+
+    @pl.when(longer)
+    def _():
+        serve[pl.ds(lo, hi - lo), :, column(me)] = late[pl.ds(0, hi - lo), peer_rows(me), :]
 
     for s in range(1, h):
         router_row(s, 0, near_back(s)).wait_recv()
@@ -250,9 +326,10 @@
         out_router[s * rows:(s + 1) * rows, :] = block.T.astype(jnp.bfloat16)
 
     for l in peers:
-        for b in range(2):
-            direct(b, l, me).wait_send()
-    for s in range(1, h):
+        direct(l, me).wait_send()
+    soon_far().wait_send()
+    for s in range(1, h):
+        soon_near(s).wait_send()
         spread(s, mine).wait_send()
         collect(s, mine).wait_send()
         router_row(s, 0, me).wait_send()
@@ -261,30 +338,133 @@
     router_swap(me).wait_send()
     for r in range(1, ne):
         router_col(r, my_e).wait_send()
+    @pl.when(longer)
+    def _():
+        for l in peers:
+            whole_piece(l, me, hi).wait_send()
+        for l in peers:
+            whole_piece(l, back(l), hi).wait_recv()
+
+    @pl.when(jnp.logical_not(longer))
+    def _():
+        for l in peers:
+            whole_piece(l, me, lo).wait_send()
+        for l in peers:
+            whole_piece(l, back(l), lo).wait_recv()
+
+
+def second(n, late, _, serve, send_sem, recv_sem):
+    me = lax.axis_index("shard")
+    my_e = lax.axis_index("expert")
+    rows = late.shape[2]
+    part = late.shape[1] // n
+    h = n // 2
+    mine = lax.rem(me, h)
+    base = me - mine
+    far = (n - h) - base
+    peers = range(n - 1)
+
+    def there(l):
+        if l < h:
+            return far + lax.rem(mine + l, h)
+        return base + lax.rem(mine + (l - h + 1), h)
+
+    def back(l):
+        if l < h:
+            return far + lax.rem(mine + (h - l), h)
+        return base + lax.rem(mine + (2 * h - 1 - l), h)
+
+    def column(slot):
+        return pl.ds(pl.multiple_of(slot * rows, LANES), rows)
+
+    def peer_rows(slot):
+        return pl.ds(pl.multiple_of(slot * part, 16), part)
+
+    def piece(l, slot, first, count):
+        return pltpu.make_async_remote_copy(
+            src_ref=late.at[pl.ds(first, count), peer_rows(there(l))],
+            dst_ref=serve.at[pl.ds(first, count), :, column(slot)],
+            send_sem=send_sem.at[l], recv_sem=recv_sem.at[l],
+            device_id={"shard": there(l)}, device_id_type=MESH,
+        )
+
+    barrier = pltpu.get_barrier_semaphore()
     for l in peers:
-        piece(l, me, 0, total).wait_send()
-    for l in peers:
-        piece(l, back(l), 0, total).wait_recv()
-
-
-def place(serve, scale, router, out_gate, out_up, out_sg, out_su, out_router, sems):
+        pl.semaphore_signal(barrier, inc=1, device_id={"shard": there(l)}, device_id_type=MESH)
+    serve[:, :, column(me)] = late[:, peer_rows(me), :]
+    pl.semaphore_wait(barrier, n - 1)
+
+    def exchange(start):
+        @pl.loop(0, (SECOND - start) // CHUNK)
+        def _(c):
+            for l in sorted(peers, key=lambda l: (l % h, l // h)):
+                piece(l, me, start + c * CHUNK, CHUNK).start()
+
+        for l in peers:
+            piece(l, me, start, SECOND - start).wait_send()
+        for l in peers:
+            piece(l, back(l), start, SECOND - start).wait_recv()
+
+    @pl.when(lax.rem(my_e, 2) == 0)
+    def _():
+        exchange(0)
+
+    @pl.when(lax.rem(my_e, 2) == 1)
+    def _():
+        exchange(SECOND - SHORT)
+
+
+def run_all(moves, sems):
+    copies = [pltpu.make_async_copy(a, b, sems.at[i]) for i, (a, b) in enumerate(moves)]
+    for copy in copies:
+        copy.start()
+    for copy in copies:
+        copy.wait()
+
+
+def place(lo, serve, scale, router, out_gate, out_up, out_sg, out_su, out_router, token, sems):
     experts = out_gate.shape[0]
     step = experts // PLACES
     moves = [
-        (serve.at[pl.ds(a * experts + i * step, step)], out.at[pl.ds(i * step, step)])
-        for a, out in enumerate((out_gate, out_up))
+        (serve.at[pl.ds(i * step, step)], out_gate.at[pl.ds(i * step, step)])
         for i in range(PLACES)
+    ]
+    rest = lo - experts
+    cuts = [rest * i // PLACES for i in range(PLACES + 1)]
+    moves += [
+        (serve.at[pl.ds(experts + a, b - a)], out_up.at[pl.ds(a, b - a)])
+        for a, b in zip(cuts, cuts[1:])
     ]
     moves += [
         (router, out_router),
         (scale.at[pl.ds(0, experts)], out_sg),
         (scale.at[pl.ds(experts, experts)], out_su),
+        (scale.at[pl.ds(0, 8)], token),
     ]
-    copies = [pltpu.make_async_copy(a, b, sems.at[i]) for i, (a, b) in enumerate(moves)]
-    for copy in copies:
-        copy.start()
-    for copy in copies:
-        copy.wait()
+    run_all(moves, sems)
+
+
+def place_second(lo, serve, tail, _, out_up, sems):
+    experts = out_up.shape[0]
+    spot = lo - experts
+    gap = SECOND - SHORT
+
+    def cut(source, at, to, count):
+        half = count // 2
+        return [
+            (source.at[pl.ds(at, half)], out_up.at[pl.ds(to, half)]),
+            (source.at[pl.ds(at + half, count - half)], out_up.at[pl.ds(to + half, count - half)]),
+        ]
+
+    longer = lax.rem(lax.axis_index("expert"), 2) == 1
+
+    @pl.when(longer)
+    def _():
+        run_all(cut(serve, lo, spot, gap) + cut(tail, gap, spot + gap, SHORT), sems)
+
+    @pl.when(jnp.logical_not(longer))
+    def _():
+        run_all(cut(tail, 0, spot, gap) + cut(tail, gap, spot + gap, SHORT), sems)
 
 
 def plain_body(w_gate, w_up, router_weight, router_gain):
@@ -317,29 +497,36 @@
     fits = (
         n % 2 == 0 and rows % LANES == 0 and cols % LANES == 0 and (cols // n) % 16 == 0
         and total > DIRECT and (total - DIRECT) % h == 0 and (total - DIRECT) % CHUNK == 0
-        and total >= SLOTS
+        and total >= SLOTS and total - SECOND >= max(experts + PLACES, DIRECT + CHUNK)
+        and (total - SECOND - DIRECT) % CHUNK == 0 and experts % PLACES == 0
     )
     if not fits:
         return plain_body(w_gate, w_up, router_weight, router_gain)
     part, share, local_e = cols // n, (total - DIRECT) // h, router_weight.shape[1]
+    lo, hi = total - SECOND, total - SHORT
     dma = pltpu.SemaphoreType.DMA
     anywhere = pl.BlockSpec(memory_space=pl.ANY)
     local = pl.BlockSpec(memory_space=pltpu.VMEM)
-    serve, scale, router = pl.pallas_call(
+    serve, late, scale, router = pl.pallas_call(
         functools.partial(kernel, n, ne),
         out_shape=(
-            pltpu.VMEM((total, part, n * rows), jnp.bfloat16),
+            pltpu.VMEM((hi, part, n * rows), jnp.bfloat16),
+            pltpu.VMEM((SECOND, cols, rows), jnp.bfloat16),
             pltpu.VMEM((total, part), jnp.float32),
             pltpu.VMEM((n * rows, ne * local_e), jnp.bfloat16),
         ),
         in_specs=[anywhere, anywhere, local, local],
-        out_specs=(local, local, local),
+        out_specs=(local, local, local, local),
         scratch_shapes=[
             pltpu.VMEM((total, 1, cols), jnp.float32),
             pltpu.VMEM((SLOTS, rows, cols), jnp.float32),
-            pltpu.VMEM((total, cols, rows), jnp.bfloat16),
+            pltpu.VMEM((NOW, cols, rows), jnp.float32),
+            pltpu.VMEM((lo, cols, rows), jnp.bfloat16),
             pltpu.VMEM((total, 1, cols), jnp.float32),
-            pltpu.VMEM((n, DIRECT, 1, cols), jnp.float32),
+            pltpu.VMEM((n, NOW, 1, cols), jnp.float32),
+            pltpu.VMEM((h, DIRECT - NOW, 1, cols), jnp.float32),
+            pltpu.VMEM((DIRECT - NOW, 1, cols), jnp.float32),
+            pltpu.VMEM((DIRECT - NOW, 1, cols), jnp.float32),
             pltpu.VMEM((h, share, 1, cols), jnp.float32),
             pltpu.VMEM((share, 1, cols), jnp.float32),
             pltpu.VMEM((share, 1, cols), jnp.float32),
@@ -347,8 +534,12 @@
             dma((SLOTS,)),
             dma((n,)),
             dma((n,)),
-            dma((2, n)),
-            dma((2, n)),
+            dma((n,)),
+            dma((n,)),
+            dma((h,)),
+            dma((h,)),
+            dma,
+            dma,
             dma((h,)),
             dma((h,)),
             dma,
@@ -363,29 +554,55 @@
             dma((ne,)),
         ],
         compiler_params=pltpu.CompilerParams(
-            collective_id=0, has_side_effects=True, vmem_limit_bytes=34 * 2**20
+            collective_id=0, has_side_effects=True, vmem_limit_bytes=30 * 2**20
         ),
         cost_estimate=pl.CostEstimate(
             flops=4 * experts * rows * cols, bytes_accessed=20 * experts * rows * cols, transcendentals=0
         ),
     )(w_gate, w_up, router_weight.T, router_gain[None, :])
-    gate, up, scale_gate, scale_up, router = pl.pallas_call(
-        place,
+    gate, up, scale_gate, scale_up, router, token = pl.pallas_call(
+        functools.partial(place, lo),
         out_shape=(
             pltpu.HBM((experts, part, n * rows), jnp.bfloat16),
             pltpu.HBM((experts, part, n * rows), jnp.bfloat16),
             pltpu.HBM((experts, part), jnp.float32),
             pltpu.HBM((experts, part), jnp.float32),
             pltpu.HBM((n * rows, ne * local_e), jnp.bfloat16),
+            pltpu.HBM((8, part), jnp.float32),
         ),
         in_specs=[local] * 3,
-        out_specs=(anywhere,) * 5,
-        scratch_shapes=[dma((2 * PLACES + 3,))],
+        out_specs=(anywhere,) * 6,
+        scratch_shapes=[dma((2 * PLACES + 4,))],
         compiler_params=pltpu.CompilerParams(vmem_limit_bytes=2**20),
         cost_estimate=pl.CostEstimate(
             flops=0, bytes_accessed=4 * experts * rows * cols, transcendentals=0
         ),
     )(serve, scale, router)
+    tail = pl.pallas_call(
+        functools.partial(second, n),
+        out_shape=pltpu.VMEM((SECOND, part, n * rows), jnp.bfloat16),
+        in_specs=[local, anywhere],
+        out_specs=local,
+        scratch_shapes=[dma((n,)), dma((n,))],
+        compiler_params=pltpu.CompilerParams(
+            collective_id=1, has_side_effects=True, vmem_limit_bytes=2**20
+        ),
+        cost_estimate=pl.CostEstimate(
+            flops=0, bytes_accessed=SECOND * rows * cols, transcendentals=0
+        ),
+    )(late, token)
+    up = pl.pallas_call(
+        functools.partial(place_second, lo),
+        out_shape=pltpu.HBM((experts, part, n * rows), jnp.bfloat16),
+        in_specs=[local, local, anywhere],
+        out_specs=anywhere,
+        input_output_aliases={2: 0},
+        scratch_shapes=[dma((4,))],
+        compiler_params=pltpu.CompilerParams(vmem_limit_bytes=2**20),
+        cost_estimate=pl.CostEstimate(
+            flops=0, bytes_accessed=4 * SECOND * rows * cols, transcendentals=0
+        ),
+    )(serve, tail, up)
     return (jnp.swapaxes(gate, 1, 2), jnp.swapaxes(up, 1, 2), scale_gate, scale_up, router)
 
 

time: 565 us -> 558 us (0.988)
  Pallas kernels: 564 us -> 557 us
    pallas_call x2 -> x4, Pallas kernels: 564 us -> 557 us  [the longest x1 439 us: body(): pl.pallas_call(functools.partial(kernel, n, ne), out_shape=(pltpu.VMEM((h...]
where the time goes in v2:
time: 558 us
  Pallas kernels  557 us (100%)
    pallas_call x1, Pallas kernels, body(): pl.pallas_call(functools.partial(kernel, n, ne), out_shape=(pltpu.VMEM((h...  439 us
    pallas_call x1, Pallas kernels, body(): pl.pallas_call(functools.partial(second, n), out_shape=pltpu.VMEM((SECOND...  108 us

profile of v2, /device:TPU:0, one launch (start us, length us, event | category | flops | bytes accessed | tf_op | source)
XLA Modules:
  0.0 557.9 jit_solution(1526145412209864484)
XLA Ops:
  0.6 438.6 %shard_map.83 = (bf16[56,96,2048]{2,1,0:T(8,128)(2,1)S(1)}, bf16[16,768,256]{2,1,0:T(8,128)(2,1)S(1)}, f32[64,96]{1,0:T(8,128)S(1)}, bf16[2048,128]{1,0:T(8,128)(2,1)S(1)}) custom-call(f32[32,256,768]{2,1,0:T(8,128)} %gate.1, f32[32,256,768]{2,1,0:T(8,128)} %up.1, f32[32,256]{1,0:T(8,128)} %bitcast.5, f32[1,256]{1,0:T(1,128)} %bitcast.6), custom_call_target="tpu_custom_call" | custom-call | flops 25165824 | bytes 125829120 | tf_op jit(solution)/shard_map/pallas_call | solution.py:510
  439.3 6.8 %shard_map.84 = (bf16[32,96,2048]{2,1,0:T(8,128)(2,1)}, bf16[32,96,2048]{2,1,0:T(8,128)(2,1)}, f32[32,96]{1,0:T(8,128)}, f32[32,96]{1,0:T(8,128)}, bf16[2048,128]{1,0:T(8,128)(2,1)}, /*index=5*/f32[8,96]{1,0:T(8,128)}) custom-call(bf16[56,96,2048]{2,1,0:T(8,128)(2,1)S(1)} %get-tuple-element.15.serve, f32[64,96]{1,0:T(8,128)S(1)} %get-tuple-element.16.scale, ...), custom_call_target="tpu_custom_call" | custom-call | bytes 25165824 | tf_op jit(solution)/shard_map/pallas_call | solution.py:563
  446.1 0.0 copy-start
  446.1 0.7 copy-done
  446.7 108.4 %shard_map.85.tail = bf16[16,96,2048]{2,1,0:T(8,128)(2,1)S(1)} custom-call(bf16[16,768,256]{2,1,0:T(8,128)(2,1)S(1)} %get-tuple-element.19.late, f32[8,96]{1,0:T(8,128)S(1)} %copy-done), custom_call_target="tpu_custom_call" | custom-call | bytes 3145728 | tf_op jit(solution)/shard_map/pallas_call | solution.py:581
  555.1 2.8 shard_map.86
Async XLA Ops:
  446.1 0.7 copy-start

commit v3 on v2

--- a/solution.py
+++ b/solution.py
@@ -13,8 +13,8 @@
 NOW = 2
 DIRECT = 8
 EARLY = 3
-SECOND = 16
-SHORT = 8
+SECOND = 10
+SHORT = 2
 CHUNK = 2
 PLACES = 8
 
@@ -395,10 +395,10 @@
     pl.semaphore_wait(barrier, n - 1)
 
     def exchange(start):
-        @pl.loop(0, (SECOND - start) // CHUNK)
+        @pl.loop(start, SECOND)
         def _(c):
             for l in sorted(peers, key=lambda l: (l % h, l // h)):
-                piece(l, me, start + c * CHUNK, CHUNK).start()
+                piece(l, me, c, 1).start()
 
         for l in peers:
             piece(l, me, start, SECOND - start).wait_send()

time: 558 us -> 557 us (level)
    pallas_call x1, Pallas kernels: 108 us -> 57.1 us  [body(): pl.pallas_call(functools.partial(second, n), out_shape=pltpu.VMEM((SECOND...]
    pallas_call x1, Pallas kernels: 439 us -> 489 us  [body(): pl.pallas_call(functools.partial(kernel, n, ne), out_shape=(pltpu.VMEM((h...]
where the time goes in v3:
time: 557 us
  Pallas kernels  556 us (100%)
    pallas_call x1, Pallas kernels, body(): pl.pallas_call(functools.partial(kernel, n, ne), out_shape=(pltpu.VMEM((h...  489 us
    pallas_call x1, Pallas kernels, body(): pl.pallas_call(functools.partial(second, n), out_shape=pltpu.VMEM((SECOND...  57.1 us

profile of v3, /device:TPU:0, one launch (start us, length us, event | category | flops | bytes accessed | tf_op | source)
XLA Modules:
  0.0 557.0 jit_solution(18092627949087891069)
XLA Ops:
  0.6 489.2 %shard_map.83 = (bf16[62,96,2048]{2,1,0:T(8,128)(2,1)S(1)}, bf16[10,768,256]{2,1,0:T(8,128)(2,1)S(1)}, f32[64,96]{1,0:T(8,128)S(1)}, bf16[2048,128]{1,0:T(8,128)(2,1)S(1)}) custom-call(f32[32,256,768]{2,1,0:T(8,128)} %gate.1, f32[32,256,768]{2,1,0:T(8,128)} %up.1, f32[32,256]{1,0:T(8,128)} %bitcast.5, f32[1,256]{1,0:T(1,128)} %bitcast.6), custom_call_target="tpu_custom_call" | custom-call | flops 25165824 | bytes 125829120 | tf_op jit(solution)/shard_map/pallas_call | solution.py:510
  489.8 7.5 %shard_map.84 = (bf16[32,96,2048]{2,1,0:T(8,128)(2,1)}, bf16[32,96,2048]{2,1,0:T(8,128)(2,1)}, f32[32,96]{1,0:T(8,128)}, f32[32,96]{1,0:T(8,128)}, bf16[2048,128]{1,0:T(8,128)(2,1)}, /*index=5*/f32[8,96]{1,0:T(8,128)}) custom-call(bf16[62,96,2048]{2,1,0:T(8,128)(2,1)S(1)} %get-tuple-element.15.serve, f32[64,96]{1,0:T(8,128)S(1)} %get-tuple-element.16.scale, ...), custom_call_target="tpu_custom_call" | custom-call | bytes 25165824 | tf_op jit(solution)/shard_map/pallas_call | solution.py:563
  497.3 0.0 copy-start
  497.3 0.7 copy-done
  498.0 57.1 %shard_map.85.tail = bf16[10,96,2048]{2,1,0:T(8,128)(2,1)S(1)} custom-call(bf16[10,768,256]{2,1,0:T(8,128)(2,1)S(1)} %get-tuple-element.19.late, f32[8,96]{1,0:T(8,128)S(1)} %copy-done), custom_call_target="tpu_custom_call" | custom-call | bytes 1966080 | tf_op jit(solution)/shard_map/pallas_call | solution.py:581
  555.1 2.0 shard_map.86
Async XLA Ops:
  497.3 0.7 copy-start
